TPU v7x, 16 devices: a whole 2x2x2 slice. The times are simulated.
16 devices in a mesh: fsdp: 16 (over z, y, x, core).
Axes of the slice: x: 2, y: 2, z: 2, core: 2. Of those that a mesh axis runs over, the one named last changes fastest.
Arguments:
- h_saved: bfloat16 [3, 32768, 896], P(None, 'fsdp')
- g_out: bfloat16 [32768, 896], P('fsdp')
- w_gate: bfloat16 [3, 896, 4864], P(None, 'fsdp')
- w_up: bfloat16 [3, 896, 4864], P(None, 'fsdp')
- w_down: bfloat16 [3, 4864, 896], P(None, 'fsdp')
Outputs:
- output 1: float32 [3, 896, 4864], P(None, 'fsdp')
- output 2: float32 [3, 896, 4864], P(None, 'fsdp')
- output 3: float32 [3, 4864, 896], P(None, 'fsdp')
- output 4: bfloat16 [32768, 896], P('fsdp')
All inputs are finite; a program needn't handle non-finite values.
Results may differ from a plain program's by a relative error of at most 0.00587019.
Values are sent between devices in bfloat16 or wider.
A program may use at most 1 GiB of HBM per device.

v0:
```python
import jax
import jax.numpy as jnp
from jax import lax
from jax.experimental import pallas as pl
from jax.experimental.pallas import tpu as pltpu
from jax.sharding import PartitionSpec as P

EPS = 1e-6
LAYERS = 3
D = 896
FF = 4864
ROWS = 2048
DEV = 16
DS = D // DEV
FS = FF // DEV
CPD = 16
CH = CPD * DEV
NC = FF // CH
NK = NC * LAYERS
LEAD = 5
TAIL = 4
WS = 6
RB = 1024
BB = 256
HALF = CH // 2
LANES = 128
NB = ROWS // BB
HR = 4
MESH = pl.DeviceIdType.MESH
BF = jnp.bfloat16
F32 = jnp.float32


def dot(a, b, ca, cb):
    return lax.dot_general(a, b, (((ca,), (cb,)), ((), ())), preferred_element_type=F32)


def kernel(h_hbm, g_hbm, w1_hbm, w3_hbm, w2_hbm,
           o1_v, o3_v, o2_v, g_v,
           n_v, nt_v, gt_v, dn_v, h_v, a_v, d_v,
           c1_v, c3_v, e1_v, e3_v, f1_v, f3_v,
           w1_v, w3_v, w2_v,
           g1_v, g3_v, g2_v,
           rd1, rd3, rd2, ra1, ra3, ra2, rb1, rb3, rb2, rc1, rc3, rc2,
           pa1, pa3, pa2, pb1, pb3, pb2, s1, s3,
           ag_send, ag_recv, rs_send, rs_recv, ex_send, ex_recv, own_sem, cols_sem, h_sem, g_sem):
    me = lax.axis_index('fsdp')
    c = me % 2
    x = (me // 2) % 2
    y = (me // 4) % 2
    z = (me // 8) % 2
    core = me + 1 - 2 * c
    nx = me + 2 - 4 * x
    ny = me + 4 - 8 * y
    nz = me + 8 - 16 * z

    weights = (w1_v, w3_v, w2_v)
    grads = (g1_v, g3_v, g2_v)
    rds, ras, rbs, rcs = (rd1, rd3, rd2), (ra1, ra3, ra2), (rb1, rb3, rb2), (rc1, rc3, rc2)
    pas, pbs, outs, dones = (pa1, pa3, pa2), (pb1, pb3, pb2), (o1_v, o3_v), (s1, s3)
    cols, halves, theirs = (c1_v, c3_v), (e1_v, e3_v), (f1_v, f3_v)
    order = ((nx, ny, nz), (ny, nz, nx), (nz, nx, ny))

    def gather_slice(m, stage, k):
        s = lax.rem(k, WS)
        w = weights[m]
        if m == 0:
            return (lambda: w.at[s, c, z, y, x], lambda: w.at[s, c, z, y], lambda: w.at[s, c, z],
                    lambda: w.at[s, c, z, y], lambda: w.at[s, c, z, 1 - y], lambda: w.at[s, c, 1 - z])[stage]()
        if m == 1:
            return (lambda: w.at[s, c, z, y, x], lambda: w.at[s, c, z, :, x], lambda: w.at[s, c, :, :, x],
                    lambda: w.at[s, c, z, :, x], lambda: w.at[s, c, 1 - z, :, x], lambda: w.at[s, c, :, :, 1 - x])[stage]()
        return (lambda: w.at[s, z, y, x, c], lambda: w.at[s, :, y, x, c], lambda: w.at[s, :, y, :, c],
                lambda: w.at[s, :, y, x, c], lambda: w.at[s, :, y, 1 - x, c], lambda: w.at[s, :, 1 - y, :, c])[stage]()

    def own_rows(k):
        return w2_hbm.at[LAYERS - 1 - k // NC, pl.ds(pl.multiple_of(lax.rem(k, NC) * CPD, CPD), CPD)]

    def gather_copy(m, stage, k):
        par = lax.rem(k, 2)
        dst = gather_slice(m, stage, k)
        src = own_rows(k) if (stage == 0 and m == 2) else dst
        peer = core if stage >= 3 else order[m][stage]
        return pltpu.make_async_remote_copy(
            src_ref=src, dst_ref=dst, send_sem=ag_send.at[m, stage, par], recv_sem=ag_recv.at[m, stage, par],
            device_id=(peer,), device_id_type=MESH)

    def own_copy(k):
        return pltpu.make_async_copy(own_rows(k), gather_slice(2, 0, k), own_sem)

    def cols_copy(m, li):
        return pltpu.make_async_copy((w1_hbm, w3_hbm)[m].at[LAYERS - 1 - li], cols[m], cols_sem.at[m])

    def half_copy(m, k):
        par = lax.rem(k, 2)
        return pltpu.make_async_remote_copy(
            src_ref=halves[m].at[par, 1 - c], dst_ref=theirs[m].at[par], send_sem=ex_send.at[m, par], recv_sem=ex_recv.at[m, par],
            device_id=(core,), device_id_type=MESH)

    lane = lax.broadcasted_iota(jnp.int32, (DS, LANES), 1)

    def place(p, i):
        col = FS * p + CPD * i
        tile = col // LANES
        return pl.ds(pl.multiple_of(tile * LANES, LANES), LANES), col - tile * LANES

    def pick_columns(k):
        i = lax.rem(k, NC)
        for m in range(2):
            for half in range(2):
                acc = jnp.zeros((DS, LANES), F32)
                for q in range(DEV // 2):
                    tile, off = place(half * (DEV // 2) + q, i)
                    part = pltpu.roll(cols[m][:, tile].astype(F32), lax.rem(CPD * q + LANES - off, LANES), 1)
                    acc = jnp.where((lane >= CPD * q) & (lane < CPD * (q + 1)), part, acc)
                halves[m][lax.rem(k, 2), half] = acc

    def merge_rows(k):
        par = lax.rem(k, 2)
        for m in range(2):
            mine, other = halves[m][par, c], theirs[m][par]
            low = jnp.where(c == 0, mine, other)
            high = jnp.where(c == 0, other, mine)
            weights[m][lax.rem(k, WS), c, z, y, x] = jnp.concatenate([low, high], axis=0).astype(BF)

    def put_columns(k):
        layer = lax.rem(LAYERS - (k + NC) // NC, LAYERS)
        i = lax.rem(k + NC, NC)
        for m in range(2):
            for half in range(2):
                src = dones[m][:, half * LANES:(half + 1) * LANES]
                for q in range(DEV // 2):
                    tile, off = place(half * (DEV // 2) + q, i)
                    part = pltpu.roll(src, lax.rem(off + LANES - CPD * q, LANES), 1)
                    outs[m][layer, :, tile] = jnp.where((lane >= off) & (lane < off + CPD), part, outs[m][layer, :, tile])

    def reduce_copy(m, stage, k):
        par = lax.rem(k, 2)
        slot = par if stage == 0 else lax.rem(k, 3)
        g, pa, pb = grads[m], pas[m].at[par], pbs[m].at[par]
        if stage == 0:
            src, dst, peer = g.at[par, :, :, :, 1 - c], rds[m].at[par], core
        elif stage == 1:
            src = (g.at[par, :, :, 1 - x, c], g.at[par, :, 1 - y, :, c], g.at[par, 1 - z, :, :, c])[m]
            dst, peer = ras[m].at[slot], order[m][0]
        elif stage == 2:
            src = (pa.at[:, 1 - y], pa.at[1 - z], pa.at[:, 1 - x])[m]
            dst, peer = rbs[m].at[slot], order[m][1]
        else:
            src = (pb.at[1 - z], pb.at[1 - x], pb.at[1 - y])[m]
            dst, peer = rcs[m].at[slot], order[m][2]
        return pltpu.make_async_remote_copy(
            src_ref=src, dst_ref=dst, send_sem=rs_send.at[m, stage, slot], recv_sem=rs_recv.at[m, stage, slot],
            device_id=(peer,), device_id_type=MESH)

    def h_copy(li, b):
        rows = pl.ds(pl.multiple_of(b * BB, BB), BB)
        slot = lax.rem(b, HR)
        return pltpu.make_async_copy(h_hbm.at[LAYERS - 1 - li, rows], h_v.at[slot], h_sem.at[slot])

    def g_copy():
        return pltpu.make_async_copy(g_hbm, g_v, g_sem)

    def finalize_rows(b):
        rows = pl.ds(pl.multiple_of(b * BB, BB), BB)
        hf = h_v[lax.rem(b, HR)].astype(F32)
        r = lax.rsqrt(jnp.mean(hf * hf, axis=-1, keepdims=True) + EPS)
        m = hf * r
        dn = dn_v[rows, :]
        dr = r * (dn - m * jnp.mean(dn * m, axis=-1, keepdims=True))
        g_v[rows, :] = (g_v[rows, :].astype(F32) + dr).astype(BF)

    def finalize_layer(li):
        def rows(b, cc):
            h_copy(li, b).wait()
            finalize_rows(b)

            @pl.when(b < NB - HR)
            def _():
                h_copy(li, b + HR).start()

            @pl.when((b >= NB - HR) & (li < LAYERS - 1))
            def _():
                h_copy(li + 1, b + HR - NB).start()
            return cc
        lax.fori_loop(0, NB, rows, 0)

    def prepare_rows(li, b):
        rows = pl.ds(pl.multiple_of(b * BB, BB), BB)
        h_copy(li, b).wait()
        hf = h_v[lax.rem(b, HR)].astype(F32)
        r = lax.rsqrt(jnp.mean(hf * hf, axis=-1, keepdims=True) + EPS)
        nb = (hf * r).astype(BF)
        n_v[rows, :] = nb
        nt_v[:, rows] = nb.T
        gt_v[:, rows] = g_v[rows, :].T
        dn_v[rows, :] = jnp.zeros((BB, D), F32)
        h_copy(li, lax.rem(b + HR, NB)).start()

    def gather_first(k):
        @pl.when((k >= 0) & (k < NK))
        def _():
            for m in range(3):
                gather_copy(m, 5, k).wait()

    def gather_rest(k):
        def live(lag):
            return (k + lag >= 0) & (k + lag < NK)

        for lag, stage in ((1, 2), (2, 1), (3, 0)):
            @pl.when(live(lag))
            def _():
                for m in range(3):
                    gather_copy(m, stage, k + lag).wait()
                    if stage > 0:
                        gather_copy(m, stage + 2, k + lag).wait()
                if stage == 0:
                    own_copy(k + lag).wait()
                for m in range(3):
                    gather_copy(m, stage + 3, k + lag).start()
                    if stage < 2:
                        gather_copy(m, stage + 1, k + lag).start()

        @pl.when(live(4))
        def _():
            for m in range(2):
                half_copy(m, k + 4).wait()
            merge_rows(k + 4)
            for m in range(3):
                gather_copy(m, 0, k + 4).start()
            own_copy(k + 4).start()

        @pl.when((k <= 0) & (k > -LEAD))
        def _():
            pick_columns(k + 5)

        @pl.when(k + 5 < NK)
        def _():
            for m in range(2):
                half_copy(m, k + 5).start()

        @pl.when((k + 6 == NC) | (k + 6 == 2 * NC))
        def _():
            for m in range(2):
                cols_copy(m, (k + 6) // NC).start()

    def reduce_step(k):
        def live(lag):
            return (k - lag >= 0) & (k - lag < NK)

        def finish():
            kf = k - 4
            for m in range(3):
                reduce_copy(m, 3, kf).wait()
            for m in range(3):
                done = rcs[m][lax.rem(kf, 3)] + pbs[m][lax.rem(kf, 2), (z, x, y)[m]]
                if m == 2:
                    o2_v[LAYERS - 1 - kf // NC, pl.ds(pl.multiple_of(lax.rem(kf, NC) * CPD, CPD), CPD), :] = done
                else:
                    dones[m][...] = done

        def third():
            kf = k - 3
            par = lax.rem(kf, 2)
            for m in range(3):
                reduce_copy(m, 2, kf).wait()
                for a in range(2):
                    kept = (lambda: pa1[par, a, y], lambda: pa3[par, z, a], lambda: pa2[par, a, x])[m]()
                    pbs[m][par, a] = rbs[m][lax.rem(kf, 3), a] + kept
                reduce_copy(m, 3, kf).start()

        def second():
            kf = k - 2
            par = lax.rem(kf, 2)
            for m in range(3):
                reduce_copy(m, 1, kf).wait()
                for a in range(2):
                    for b in range(2):
                        kept = (lambda: g1_v[par, a, b, x, c], lambda: g3_v[par, a, y, b, c], lambda: g2_v[par, z, a, b, c])[m]()
                        pas[m][par, a, b] = ras[m][lax.rem(kf, 3), a, b] + kept
                reduce_copy(m, 2, kf).start()

        def first():
            kf = k - 1
            par = lax.rem(kf, 2)
            for m in range(3):
                reduce_copy(m, 0, kf).wait()
                for a in range(2):
                    for b in range(2):
                        for d in range(2):
                            grads[m][par, a, b, d, c] = grads[m][par, a, b, d, c] + rds[m][par, a, b, d]
                reduce_copy(m, 1, kf).start()

        @pl.when((k + 6 == NC) | (k + 6 == 2 * NC))
        def _():
            for m in range(2):
                cols_copy(m, (k + 6) // NC).wait()

        @pl.when(k <= NK)
        def _():
            pl.when(live(4))(finish)

        @pl.when(k < NK)
        def _():
            pl.when(live(3))(third)
            pl.when(live(2))(second)
            pl.when(live(1))(first)

        @pl.when(k >= NK)
        def _():
            pl.when(live(1))(first)
            pl.when(k == NK)(lambda: finalize_layer(LAYERS - 1))
            pl.when(live(2))(second)
            pl.when(live(3))(third)

        @pl.when(k > NK)
        def _():
            finish()

    def row_phase(k):
        s = lax.rem(k, WS)

        def body(b, carry):
            @pl.when((k == 0) & (b == 1))
            def _():
                gather_rest(k)

            rows = pl.ds(pl.multiple_of(b * RB, RB), RB)
            w1 = jnp.concatenate([w1_v[s, 0].reshape(D, HALF), w1_v[s, 1].reshape(D, HALF)], axis=1)
            w3 = jnp.concatenate([w3_v[s, 0].reshape(D, HALF), w3_v[s, 1].reshape(D, HALF)], axis=1)
            w2 = w2_v[s].reshape(CH, D)
            nb = n_v[rows, :]
            u = dot(nb, w1, 1, 0)
            v = dot(nb, w3, 1, 0)
            da = jnp.concatenate([dot(g_v[pl.ds(pl.multiple_of(b * RB + q * (RB // 2), RB // 2), RB // 2), :], w2, 1, 1) for q in range(2)], axis=0)
            sig = 1.0 / (1.0 + jnp.exp(-u))
            act = u * sig
            a_v[rows, :] = (act * v).astype(BF)
            du = (da * v * sig * (1.0 + u * (1.0 - sig))).astype(BF)
            dv = (da * act).astype(BF)
            d_v[rows, pl.ds(0, CH)] = du
            d_v[rows, pl.ds(CH, CH)] = dv
            for q in range(2):
                rq = slice(q * (RB // 2), (q + 1) * (RB // 2))
                rr = pl.ds(pl.multiple_of(b * RB + q * (RB // 2), RB // 2), RB // 2)
                dn_v[rr, :] += dot(du[rq], w1, 1, 1) + dot(dv[rq], w3, 1, 1)
            return carry

        lax.fori_loop(0, ROWS // RB, body, 0)

    def grad_phase(k):
        par = lax.rem(k, 2)
        pick_columns(k + 6)
        put_columns(k - 4)
        nt = nt_v[...]
        g1_v[par] = dot(nt, d_v[:, pl.ds(0, CH)], 1, 0).reshape(2, 2, 2, 2, DS, CH)
        g3_v[par] = dot(nt, d_v[:, pl.ds(CH, CH)], 1, 0).reshape(2, 2, 2, 2, DS, CH)
        g2_v[par] = dot(gt_v[...], a_v[...], 1, 0).T.reshape(2, 2, 2, 2, CPD, D)

    for m in range(2):
        cols_copy(m, 0).start()
    barrier = pltpu.get_barrier_semaphore()
    for peer in (core, nx, ny, nz):
        pl.semaphore_signal(barrier, inc=1, device_id=(peer,), device_id_type=MESH)
    for b in range(HR):
        h_copy(0, b).start()
    g_copy().start()
    for m in range(2):
        cols_copy(m, 0).wait()
    pick_columns(0)
    pl.semaphore_wait(barrier, 4)

    def step(t, carry):
        k = t - LEAD
        inside = (k >= 0) & (k < NK)
        last = inside & (lax.rem(k + NC, NC) == NC - 1)
        gather_first(k)

        @pl.when(k != 0)
        def _():
            gather_rest(k)

        @pl.when((t >= 1) & (t < LEAD))
        def _():
            @pl.when(t == 1)
            def _():
                g_copy().wait()

            def rows(b, cc):
                prepare_rows(0, b)
                return cc
            lax.fori_loop(3 * (t - 1), 3 * t - t // 3 - t // 4 * 3, rows, 0)

        @pl.when(inside)
        def _():
            row_phase(k)

        @pl.when(last & (k < NK - 1))
        def _():
            finalize_layer(k // NC)

        reduce_step(k)

        @pl.when(inside)
        def _():
            grad_phase(k)
            for m in range(3):
                reduce_copy(m, 0, k).start()

        @pl.when(k >= NK)
        def _():
            put_columns(k - 4)

        @pl.when(last & (k < NK - 1))
        def _():
            li = k // NC

            def rows(b, cc):
                prepare_rows(li + 1, b)
                return cc
            lax.fori_loop(0, NB, rows, 0)
        return carry

    lax.fori_loop(0, LEAD + NK + TAIL, step, 0)


def hand_out(*refs):
    srcs, dsts, sem = refs[:4], refs[4:8], refs[8]
    pieces = [(j, layer) for j in range(3) for layer in range(LAYERS)]
    pieces += [(3, pl.ds(q * (ROWS // 4), ROWS // 4)) for q in range(4)]
    copies = [pltpu.make_async_copy(srcs[j].at[w], dsts[j].at[w], sem.at[n]) for n, (j, w) in enumerate(pieces)]
    for copy in copies:
        copy.start()
    for copy in copies:
        copy.wait()


def fused(h, g, w1, w3, w2):
    any_spec = pl.BlockSpec(memory_space=pl.ANY)
    V = pltpu.VMEM
    wide, low = (DS, CH), (CPD, D)
    three = lambda *lead: [V(lead + wide, F32), V(lead + wide, F32), V(lead + low, F32)]
    scratch = [
        V((ROWS, D), BF), V((D, ROWS), BF), V((D, ROWS), BF),
        V((ROWS, D), F32), V((HR, BB, D), BF), V((ROWS, CH), BF), V((ROWS, 2 * CH), BF),
        V((DS, FF), BF), V((DS, FF), BF), V((2, 2, DS, LANES), F32), V((2, 2, DS, LANES), F32),
        V((2, DS, LANES), F32), V((2, DS, LANES), F32),
        V((WS, 2, 2, 2, 2, 2 * DS, HALF), BF), V((WS, 2, 2, 2, 2, 2 * DS, HALF), BF), V((WS, 2, 2, 2, 2, CPD, D), BF),
        *three(2, 2, 2, 2, 2),
        *three(2, 2, 2, 2), *three(3, 2, 2), *three(3, 2), *three(3),
        *three(2, 2, 2), *three(2, 2), V(wide, F32), V(wide, F32),
        pltpu.SemaphoreType.DMA((3, 6, 2)), pltpu.SemaphoreType.DMA((3, 6, 2)),
        pltpu.SemaphoreType.DMA((3, 4, 3)), pltpu.SemaphoreType.DMA((3, 4, 3)),
        pltpu.SemaphoreType.DMA((2, 2)), pltpu.SemaphoreType.DMA((2, 2)),
        pltpu.SemaphoreType.DMA(()), pltpu.SemaphoreType.DMA((2,)),
        pltpu.SemaphoreType.DMA((HR,)), pltpu.SemaphoreType.DMA(()),
    ]
    results = (
        jax.ShapeDtypeStruct((LAYERS, DS, FF), F32),
        jax.ShapeDtypeStruct((LAYERS, DS, FF), F32),
        jax.ShapeDtypeStruct((LAYERS, FS, D), F32),
        jax.ShapeDtypeStruct((ROWS, D), BF),
    )
    vmem_spec = pl.BlockSpec(memory_space=pltpu.VMEM)
    parts = pl.pallas_call(
        kernel,
        name='mlp_backward',
        out_shape=tuple(V(r.shape, r.dtype) for r in results),
        in_specs=[any_spec] * 5,
        out_specs=(vmem_spec,) * 4,
        scratch_shapes=scratch,
        compiler_params=pltpu.CompilerParams(collective_id=0, has_side_effects=True, vmem_limit_bytes=51 * 1024 * 1024),
    )(h, g, w1, w3, w2)
    return pl.pallas_call(
        hand_out,
        name='hand_out',
        out_shape=results,
        in_specs=[vmem_spec] * 4,
        out_specs=(any_spec,) * 4,
        scratch_shapes=[pltpu.SemaphoreType.DMA((13,))],
        compiler_params=pltpu.CompilerParams(vmem_limit_bytes=1024 * 1024),
    )(*[pltpu.with_memory_space_constraint(part, pltpu.VMEM) for part in parts])


def solution(mesh):
    weight_spec = P(None, 'fsdp', None)
    row_spec = P('fsdp', None)

    return jax.shard_map(fused, mesh=mesh, in_specs=(weight_spec, row_spec, weight_spec, weight_spec, weight_spec), out_specs=(weight_spec, weight_spec, weight_spec, row_spec), check_vma=False)
```

profile of v0, /device:TPU:0, one launch (start us, length us, event | category | flops | bytes accessed | tf_op | source)
XLA Modules:
  0.0 762.2 jit_solution(18162435213357077603)
XLA Ops:
  0.6 756.6 %mlp_backward.1 = (f32[3,56,4864]{2,1,0:T(8,128)S(1)}, f32[3,56,4864]{2,1,0:T(8,128)S(1)}, f32[3,304,896]{2,1,0:T(8,128)S(1)}, bf16[2048,896]{1,0:T(8,128)(2,1)S(1)}) custom-call(bf16[3,2048,896]{2,1,0:T(8,128)(2,1)} %h_hbm.1, bf16[2048,896]{1,0:T(8,128)(2,1)} %g_hbm.1, bf16[3,56,4864]{2,1,0:T(8,128)(2,1)} %w1_hbm.1, bf16[3,56,4864]{2,1,0:T(8,128)(2,1)} %w3_hbm.1, ...), custom_call_target="tpu_custom_call" | custom-call | tf_op jit(solution)/shard_map/mlp_backward/pallas_call | solution.py:465
  757.3 4.9 hand_out.1
where the time goes:
time: 762 us
  Pallas kernels  762 us (100%)
    pallas_call x1, Pallas kernels, fused(): pl.pallas_call(kernel, name='mlp_backward', out_shape=tuple((V(r.shape, r...  757 us

commit v1 on v0

--- a/solution.py
+++ b/solution.py
@@ -79,10 +79,9 @@
     def gather_copy(m, stage, k):
         par = lax.rem(k, 2)
         dst = gather_slice(m, stage, k)
-        src = own_rows(k) if (stage == 0 and m == 2) else dst
         peer = core if stage >= 3 else order[m][stage]
         return pltpu.make_async_remote_copy(
-            src_ref=src, dst_ref=dst, send_sem=ag_send.at[m, stage, par], recv_sem=ag_recv.at[m, stage, par],
+            src_ref=dst, dst_ref=dst, send_sem=ag_send.at[m, stage, par], recv_sem=ag_recv.at[m, stage, par],
             device_id=(peer,), device_id_type=MESH)
 
     def own_copy(k):
@@ -214,8 +213,6 @@
                     gather_copy(m, stage, k + lag).wait()
                     if stage > 0:
                         gather_copy(m, stage + 2, k + lag).wait()
-                if stage == 0:
-                    own_copy(k + lag).wait()
                 for m in range(3):
                     gather_copy(m, stage + 3, k + lag).start()
                     if stage < 2:
@@ -226,9 +223,9 @@
             for m in range(2):
                 half_copy(m, k + 4).wait()
             merge_rows(k + 4)
+            own_copy(k + 4).wait()
             for m in range(3):
                 gather_copy(m, 0, k + 4).start()
-            own_copy(k + 4).start()
 
         @pl.when((k <= 0) & (k > -LEAD))
         def _():
@@ -236,6 +233,7 @@
 
         @pl.when(k + 5 < NK)
         def _():
+            own_copy(k + 5).start()
             for m in range(2):
                 half_copy(m, k + 5).start()
 

time: 762 us -> 763 us (level)
  no operation moved by 1% of the time
where the time goes in v1:
time: 763 us; the launch traced here: 762 us
  Pallas kernels  762 us (100%)
    pallas_call x1, Pallas kernels, fused(): pl.pallas_call(kernel, name='mlp_backward', out_shape=tuple((V(r.shape, r...  757 us

profile of v1, /device:TPU:0, one launch (start us, length us, event | category | flops | bytes accessed | tf_op | source)
XLA Modules:
  0.0 762.4 jit_solution(17077881065754690571)
XLA Ops:
  0.6 756.8 %mlp_backward.1 = (f32[3,56,4864]{2,1,0:T(8,128)S(1)}, f32[3,56,4864]{2,1,0:T(8,128)S(1)}, f32[3,304,896]{2,1,0:T(8,128)S(1)}, bf16[2048,896]{1,0:T(8,128)(2,1)S(1)}) custom-call(bf16[3,2048,896]{2,1,0:T(8,128)(2,1)} %h_hbm.1, bf16[2048,896]{1,0:T(8,128)(2,1)} %g_hbm.1, bf16[3,56,4864]{2,1,0:T(8,128)(2,1)} %w1_hbm.1, bf16[3,56,4864]{2,1,0:T(8,128)(2,1)} %w3_hbm.1, ...), custom_call_target="tpu_custom_call" | custom-call | tf_op jit(solution)/shard_map/mlp_backward/pallas_call | solution.py:463
  757.4 4.9 hand_out.1

commit v2 on v0

--- a/solution.py
+++ b/solution.py
@@ -82,8 +82,27 @@
         src = own_rows(k) if (stage == 0 and m == 2) else dst
         peer = core if stage >= 3 else order[m][stage]
         return pltpu.make_async_remote_copy(
-            src_ref=src, dst_ref=dst, send_sem=ag_send.at[m, stage, par], recv_sem=ag_recv.at[m, stage, par],
+            src_ref=src, dst_ref=dst, send_sem=ag_send.at[stage, par], recv_sem=ag_recv.at[stage, par],
             device_id=(peer,), device_id_type=MESH)
+
+    def wait_bytes(ref, *sems):
+        for sem in sems:
+            pltpu.make_async_copy(ref, ref, sem).wait()
+
+    def gather_wait(stage, k):
+        par = lax.rem(k, 2)
+        three = w1_v.at[pl.ds(0, 3)]
+        blocks = (three.at[:, 0, 0, 0, 0], three.at[:, 0, 0, 0], three.at[:, 0, 0])[(0, 1, 2, 1, 1, 2)[stage]]
+        wait_bytes(blocks, ag_send.at[stage, par], ag_recv.at[stage, par])
+
+    def reduce_wait(stage, k):
+        slot = lax.rem(k, 2 if stage == 0 else 3)
+        blocks = (w1_v.at[pl.ds(0, 3)], ra1, ra1.at[:, 0], ra1.at[:, 0, 0])[stage]
+        wait_bytes(blocks, rs_send.at[stage, slot], rs_recv.at[stage, slot])
+
+    def half_wait(k):
+        par = lax.rem(k, 2)
+        wait_bytes(f1_v, ex_send.at[par], ex_recv.at[par])
 
     def own_copy(k):
         return pltpu.make_async_copy(own_rows(k), gather_slice(2, 0, k), own_sem)
@@ -94,7 +113,7 @@
     def half_copy(m, k):
         par = lax.rem(k, 2)
         return pltpu.make_async_remote_copy(
-            src_ref=halves[m].at[par, 1 - c], dst_ref=theirs[m].at[par], send_sem=ex_send.at[m, par], recv_sem=ex_recv.at[m, par],
+            src_ref=halves[m].at[par, 1 - c], dst_ref=theirs[m].at[par], send_sem=ex_send.at[par], recv_sem=ex_recv.at[par],
             device_id=(core,), device_id_type=MESH)
 
     lane = lax.broadcasted_iota(jnp.int32, (DS, LANES), 1)
@@ -150,7 +169,7 @@
             src = (pb.at[1 - z], pb.at[1 - x], pb.at[1 - y])[m]
             dst, peer = rcs[m].at[slot], order[m][2]
         return pltpu.make_async_remote_copy(
-            src_ref=src, dst_ref=dst, send_sem=rs_send.at[m, stage, slot], recv_sem=rs_recv.at[m, stage, slot],
+            src_ref=src, dst_ref=dst, send_sem=rs_send.at[stage, slot], recv_sem=rs_recv.at[stage, slot],
             device_id=(peer,), device_id_type=MESH)
 
     def h_copy(li, b):
@@ -200,8 +219,7 @@
     def gather_first(k):
         @pl.when((k >= 0) & (k < NK))
         def _():
-            for m in range(3):
-                gather_copy(m, 5, k).wait()
+            gather_wait(5, k)
 
     def gather_rest(k):
         def live(lag):
@@ -210,10 +228,9 @@
         for lag, stage in ((1, 2), (2, 1), (3, 0)):
             @pl.when(live(lag))
             def _():
-                for m in range(3):
-                    gather_copy(m, stage, k + lag).wait()
-                    if stage > 0:
-                        gather_copy(m, stage + 2, k + lag).wait()
+                gather_wait(stage, k + lag)
+                if stage > 0:
+                    gather_wait(stage + 2, k + lag)
                 if stage == 0:
                     own_copy(k + lag).wait()
                 for m in range(3):
@@ -223,8 +240,7 @@
 
         @pl.when(live(4))
         def _():
-            for m in range(2):
-                half_copy(m, k + 4).wait()
+            half_wait(k + 4)
             merge_rows(k + 4)
             for m in range(3):
                 gather_copy(m, 0, k + 4).start()
@@ -250,8 +266,7 @@
 
         def finish():
             kf = k - 4
-            for m in range(3):
-                reduce_copy(m, 3, kf).wait()
+            reduce_wait(3, kf)
             for m in range(3):
                 done = rcs[m][lax.rem(kf, 3)] + pbs[m][lax.rem(kf, 2), (z, x, y)[m]]
                 if m == 2:
@@ -262,8 +277,8 @@
         def third():
             kf = k - 3
             par = lax.rem(kf, 2)
+            reduce_wait(2, kf)
             for m in range(3):
-                reduce_copy(m, 2, kf).wait()
                 for a in range(2):
                     kept = (lambda: pa1[par, a, y], lambda: pa3[par, z, a], lambda: pa2[par, a, x])[m]()
                     pbs[m][par, a] = rbs[m][lax.rem(kf, 3), a] + kept
@@ -272,8 +287,8 @@
         def second():
             kf = k - 2
             par = lax.rem(kf, 2)
+            reduce_wait(1, kf)
             for m in range(3):
-                reduce_copy(m, 1, kf).wait()
                 for a in range(2):
                     for b in range(2):
                         kept = (lambda: g1_v[par, a, b, x, c], lambda: g3_v[par, a, y, b, c], lambda: g2_v[par, z, a, b, c])[m]()
@@ -283,8 +298,8 @@
         def first():
             kf = k - 1
             par = lax.rem(kf, 2)
+            reduce_wait(0, kf)
             for m in range(3):
-                reduce_copy(m, 0, kf).wait()
                 for a in range(2):
                     for b in range(2):
                         for d in range(2):
@@ -449,9 +464,9 @@
         *three(2, 2, 2, 2, 2),
         *three(2, 2, 2, 2), *three(3, 2, 2), *three(3, 2), *three(3),
         *three(2, 2, 2), *three(2, 2), V(wide, F32), V(wide, F32),
-        pltpu.SemaphoreType.DMA((3, 6, 2)), pltpu.SemaphoreType.DMA((3, 6, 2)),
-        pltpu.SemaphoreType.DMA((3, 4, 3)), pltpu.SemaphoreType.DMA((3, 4, 3)),
-        pltpu.SemaphoreType.DMA((2, 2)), pltpu.SemaphoreType.DMA((2, 2)),
+        pltpu.SemaphoreType.DMA((6, 2)), pltpu.SemaphoreType.DMA((6, 2)),
+        pltpu.SemaphoreType.DMA((4, 3)), pltpu.SemaphoreType.DMA((4, 3)),
+        pltpu.SemaphoreType.DMA((2,)), pltpu.SemaphoreType.DMA((2,)),
         pltpu.SemaphoreType.DMA(()), pltpu.SemaphoreType.DMA((2,)),
         pltpu.SemaphoreType.DMA((HR,)), pltpu.SemaphoreType.DMA(()),
     ]

time: 762 us -> 761 us (level)
  no operation moved by 1% of the time
where the time goes in v2:
time: 761 us
  Pallas kernels  760 us (100%)
    pallas_call x1, Pallas kernels, fused(): pl.pallas_call(kernel, name='mlp_backward', out_shape=tuple((V(r.shape, r...  756 us

profile of v2, /device:TPU:0, one launch (start us, length us, event | category | flops | bytes accessed | tf_op | source)
XLA Modules:
  0.0 761.1 jit_solution(9215981986080088487)
XLA Ops:
  0.6 755.5 %mlp_backward.1 = (f32[3,56,4864]{2,1,0:T(8,128)S(1)}, f32[3,56,4864]{2,1,0:T(8,128)S(1)}, f32[3,304,896]{2,1,0:T(8,128)S(1)}, bf16[2048,896]{1,0:T(8,128)(2,1)S(1)}) custom-call(bf16[3,2048,896]{2,1,0:T(8,128)(2,1)} %h_hbm.1, bf16[2048,896]{1,0:T(8,128)(2,1)} %g_hbm.1, bf16[3,56,4864]{2,1,0:T(8,128)(2,1)} %w1_hbm.1, bf16[3,56,4864]{2,1,0:T(8,128)(2,1)} %w3_hbm.1, ...), custom_call_target="tpu_custom_call" | custom-call | tf_op jit(solution)/shard_map/mlp_backward/pallas_call | solution.py:480
  756.2 4.9 hand_out.1

commit v3 on v2

--- a/solution.py
+++ b/solution.py
@@ -96,9 +96,9 @@
         wait_bytes(blocks, ag_send.at[stage, par], ag_recv.at[stage, par])
 
     def reduce_wait(stage, k):
-        slot = lax.rem(k, 2 if stage == 0 else 3)
+        sem = lax.rem(k, 2 if stage == 0 else 3) + (0, 2, 5, 8)[stage]
         blocks = (w1_v.at[pl.ds(0, 3)], ra1, ra1.at[:, 0], ra1.at[:, 0, 0])[stage]
-        wait_bytes(blocks, rs_send.at[stage, slot], rs_recv.at[stage, slot])
+        wait_bytes(blocks, rs_send.at[sem], rs_recv.at[sem])
 
     def half_wait(k):
         par = lax.rem(k, 2)
@@ -113,7 +113,7 @@
     def half_copy(m, k):
         par = lax.rem(k, 2)
         return pltpu.make_async_remote_copy(
-            src_ref=halves[m].at[par, 1 - c], dst_ref=theirs[m].at[par], send_sem=ex_send.at[par], recv_sem=ex_recv.at[par],
+            src_ref=halves[m].at[lax.rem(k, 3), 1 - c], dst_ref=theirs[m].at[par], send_sem=ex_send.at[par], recv_sem=ex_recv.at[par],
             device_id=(core,), device_id_type=MESH)
 
     lane = lax.broadcasted_iota(jnp.int32, (DS, LANES), 1)
@@ -132,12 +132,12 @@
                     tile, off = place(half * (DEV // 2) + q, i)
                     part = pltpu.roll(cols[m][:, tile].astype(F32), lax.rem(CPD * q + LANES - off, LANES), 1)
                     acc = jnp.where((lane >= CPD * q) & (lane < CPD * (q + 1)), part, acc)
-                halves[m][lax.rem(k, 2), half] = acc
+                halves[m][lax.rem(k, 3), half] = acc
 
     def merge_rows(k):
         par = lax.rem(k, 2)
         for m in range(2):
-            mine, other = halves[m][par, c], theirs[m][par]
+            mine, other = halves[m][lax.rem(k, 3), c], theirs[m][par]
             low = jnp.where(c == 0, mine, other)
             high = jnp.where(c == 0, other, mine)
             weights[m][lax.rem(k, WS), c, z, y, x] = jnp.concatenate([low, high], axis=0).astype(BF)
@@ -156,6 +156,7 @@
     def reduce_copy(m, stage, k):
         par = lax.rem(k, 2)
         slot = par if stage == 0 else lax.rem(k, 3)
+        sem = slot + (0, 2, 5, 8)[stage]
         g, pa, pb = grads[m], pas[m].at[par], pbs[m].at[par]
         if stage == 0:
             src, dst, peer = g.at[par, :, :, :, 1 - c], rds[m].at[par], core
@@ -169,7 +170,7 @@
             src = (pb.at[1 - z], pb.at[1 - x], pb.at[1 - y])[m]
             dst, peer = rcs[m].at[slot], order[m][2]
         return pltpu.make_async_remote_copy(
-            src_ref=src, dst_ref=dst, send_sem=rs_send.at[stage, slot], recv_sem=rs_recv.at[stage, slot],
+            src_ref=src, dst_ref=dst, send_sem=rs_send.at[sem], recv_sem=rs_recv.at[sem],
             device_id=(peer,), device_id_type=MESH)
 
     def h_copy(li, b):
@@ -246,14 +247,18 @@
                 gather_copy(m, 0, k + 4).start()
             own_copy(k + 4).start()
 
-        @pl.when((k <= 0) & (k > -LEAD))
-        def _():
-            pick_columns(k + 5)
-
         @pl.when(k + 5 < NK)
         def _():
             for m in range(2):
                 half_copy(m, k + 5).start()
+
+        @pl.when(k < -3)
+        def _():
+            pick_columns(k + 6)
+
+        @pl.when((k >= -4) & (k < -1))
+        def _():
+            pick_columns(k + 7)
 
         @pl.when((k + 6 == NC) | (k + 6 == 2 * NC))
         def _():
@@ -441,8 +446,11 @@
 
 def hand_out(*refs):
     srcs, dsts, sem = refs[:4], refs[4:8], refs[8]
-    pieces = [(j, layer) for j in range(3) for layer in range(LAYERS)]
-    pieces += [(3, pl.ds(q * (ROWS // 4), ROWS // 4)) for q in range(4)]
+    pieces = []
+    for j, cut in enumerate((DS * 3 // 7, DS * 3 // 7, FS // 2)):
+        for layer in range(LAYERS):
+            pieces += [(j, (layer, pl.ds(0, cut))), (j, (layer, pl.ds(cut, srcs[j].shape[1] - cut)))]
+    pieces += [(3, pl.ds(q * (ROWS // 8), ROWS // 8)) for q in range(8)]
     copies = [pltpu.make_async_copy(srcs[j].at[w], dsts[j].at[w], sem.at[n]) for n, (j, w) in enumerate(pieces)]
     for copy in copies:
         copy.start()
@@ -458,14 +466,14 @@
     scratch = [
         V((ROWS, D), BF), V((D, ROWS), BF), V((D, ROWS), BF),
         V((ROWS, D), F32), V((HR, BB, D), BF), V((ROWS, CH), BF), V((ROWS, 2 * CH), BF),
-        V((DS, FF), BF), V((DS, FF), BF), V((2, 2, DS, LANES), F32), V((2, 2, DS, LANES), F32),
+        V((DS, FF), BF), V((DS, FF), BF), V((3, 2, DS, LANES), F32), V((3, 2, DS, LANES), F32),
         V((2, DS, LANES), F32), V((2, DS, LANES), F32),
         V((WS, 2, 2, 2, 2, 2 * DS, HALF), BF), V((WS, 2, 2, 2, 2, 2 * DS, HALF), BF), V((WS, 2, 2, 2, 2, CPD, D), BF),
         *three(2, 2, 2, 2, 2),
         *three(2, 2, 2, 2), *three(3, 2, 2), *three(3, 2), *three(3),
         *three(2, 2, 2), *three(2, 2), V(wide, F32), V(wide, F32),
         pltpu.SemaphoreType.DMA((6, 2)), pltpu.SemaphoreType.DMA((6, 2)),
-        pltpu.SemaphoreType.DMA((4, 3)), pltpu.SemaphoreType.DMA((4, 3)),
+        pltpu.SemaphoreType.DMA((11,)), pltpu.SemaphoreType.DMA((11,)),
         pltpu.SemaphoreType.DMA((2,)), pltpu.SemaphoreType.DMA((2,)),
         pltpu.SemaphoreType.DMA(()), pltpu.SemaphoreType.DMA((2,)),
         pltpu.SemaphoreType.DMA((HR,)), pltpu.SemaphoreType.DMA(()),
@@ -492,7 +500,7 @@
         out_shape=results,
         in_specs=[vmem_spec] * 4,
         out_specs=(any_spec,) * 4,
-        scratch_shapes=[pltpu.SemaphoreType.DMA((13,))],
+        scratch_shapes=[pltpu.SemaphoreType.DMA((26,))],
         compiler_params=pltpu.CompilerParams(vmem_limit_bytes=1024 * 1024),
     )(*[pltpu.with_memory_space_constraint(part, pltpu.VMEM) for part in parts])
 

time: 761 us -> 763 us (level)
  no operation moved by 1% of the time
where the time goes in v3:
time: 763 us; the launch traced here: 762 us
  Pallas kernels  762 us (100%)
    pallas_call x1, Pallas kernels, fused(): pl.pallas_call(kernel, name='mlp_backward', out_shape=tuple((V(r.shape, r...  757 us

profile of v3, /device:TPU:0, one launch (start us, length us, event | category | flops | bytes accessed | tf_op | source)
XLA Modules:
  0.0 762.4 jit_solution(8474990842762481021)
XLA Ops:
  0.6 756.7 %mlp_backward.1 = (f32[3,56,4864]{2,1,0:T(8,128)S(1)}, f32[3,56,4864]{2,1,0:T(8,128)S(1)}, f32[3,304,896]{2,1,0:T(8,128)S(1)}, bf16[2048,896]{1,0:T(8,128)(2,1)S(1)}) custom-call(bf16[3,2048,896]{2,1,0:T(8,128)(2,1)} %h_hbm.1, bf16[2048,896]{1,0:T(8,128)(2,1)} %g_hbm.1, bf16[3,56,4864]{2,1,0:T(8,128)(2,1)} %w1_hbm.1, bf16[3,56,4864]{2,1,0:T(8,128)(2,1)} %w3_hbm.1, ...), custom_call_target="tpu_custom_call" | custom-call | tf_op jit(solution)/shard_map/mlp_backward/pallas_call | solution.py:488
  757.4 5.0 hand_out.1

commit v4 on v2

--- a/solution.py
+++ b/solution.py
@@ -156,7 +156,7 @@
     def reduce_copy(m, stage, k):
         par = lax.rem(k, 2)
         slot = par if stage == 0 else lax.rem(k, 3)
-        g, pa, pb = grads[m], pas[m].at[par], pbs[m].at[par]
+        g, pa, pb = grads[m], pas[m].at[par], pbs[m].at[lax.rem(k, 3)]
         if stage == 0:
             src, dst, peer = g.at[par, :, :, :, 1 - c], rds[m].at[par], core
         elif stage == 1:
@@ -264,28 +264,26 @@
         def live(lag):
             return (k - lag >= 0) & (k - lag < NK)
 
-        def finish():
-            kf = k - 4
+        def finish(kf):
             reduce_wait(3, kf)
             for m in range(3):
-                done = rcs[m][lax.rem(kf, 3)] + pbs[m][lax.rem(kf, 2), (z, x, y)[m]]
+                done = rcs[m][lax.rem(kf, 3)] + pbs[m][lax.rem(kf, 3), (z, x, y)[m]]
                 if m == 2:
                     o2_v[LAYERS - 1 - kf // NC, pl.ds(pl.multiple_of(lax.rem(kf, NC) * CPD, CPD), CPD), :] = done
                 else:
                     dones[m][...] = done
 
-        def third():
-            kf = k - 3
+        def third(kf, send=True):
             par = lax.rem(kf, 2)
             reduce_wait(2, kf)
             for m in range(3):
                 for a in range(2):
                     kept = (lambda: pa1[par, a, y], lambda: pa3[par, z, a], lambda: pa2[par, a, x])[m]()
-                    pbs[m][par, a] = rbs[m][lax.rem(kf, 3), a] + kept
-                reduce_copy(m, 3, kf).start()
-
-        def second():
-            kf = k - 2
+                    pbs[m][lax.rem(kf, 3), a] = rbs[m][lax.rem(kf, 3), a] + kept
+                if send:
+                    reduce_copy(m, 3, kf).start()
+
+        def second(kf):
             par = lax.rem(kf, 2)
             reduce_wait(1, kf)
             for m in range(3):
@@ -295,8 +293,7 @@
                         pas[m][par, a, b] = ras[m][lax.rem(kf, 3), a, b] + kept
                 reduce_copy(m, 2, kf).start()
 
-        def first():
-            kf = k - 1
+        def first(kf):
             par = lax.rem(kf, 2)
             reduce_wait(0, kf)
             for m in range(3):
@@ -313,24 +310,40 @@
 
         @pl.when(k <= NK)
         def _():
-            pl.when(live(4))(finish)
+            pl.when(live(4))(lambda: finish(k - 4))
 
         @pl.when(k < NK)
         def _():
-            pl.when(live(3))(third)
-            pl.when(live(2))(second)
-            pl.when(live(1))(first)
-
-        @pl.when(k >= NK)
-        def _():
-            pl.when(live(1))(first)
-            pl.when(k == NK)(lambda: finalize_layer(LAYERS - 1))
-            pl.when(live(2))(second)
-            pl.when(live(3))(third)
-
-        @pl.when(k > NK)
-        def _():
-            finish()
+            pl.when(live(3))(lambda: third(k - 3))
+            pl.when(live(2))(lambda: second(k - 2))
+            pl.when(live(1))(lambda: first(k - 1))
+
+        @pl.when(k == NK)
+        def _():
+            first(k - 1)
+            finalize_layer(LAYERS - 1)
+            second(k - 2)
+            third(k - 3, send=False)
+
+        @pl.when(k == NK + 1)
+        def _():
+            second(k - 2)
+            for m in range(3):
+                reduce_copy(m, 3, k - 4).start()
+            third(k - 3)
+
+        @pl.when(k == NK + 2)
+        def _():
+            third(k - 3)
+            finish(k - 5)
+            put_columns(k - 5)
+            finish(k - 4)
+            put_columns(k - 4)
+
+        @pl.when(k == NK + 3)
+        def _():
+            finish(k - 4)
+            put_columns(k - 4)
 
     def row_phase(k):
         s = lax.rem(k, WS)
@@ -422,7 +435,7 @@
             for m in range(3):
                 reduce_copy(m, 0, k).start()
 
-        @pl.when(k >= NK)
+        @pl.when(k == NK)
         def _():
             put_columns(k - 4)
 
@@ -463,7 +476,7 @@
         V((WS, 2, 2, 2, 2, 2 * DS, HALF), BF), V((WS, 2, 2, 2, 2, 2 * DS, HALF), BF), V((WS, 2, 2, 2, 2, CPD, D), BF),
         *three(2, 2, 2, 2, 2),
         *three(2, 2, 2, 2), *three(3, 2, 2), *three(3, 2), *three(3),
-        *three(2, 2, 2), *three(2, 2), V(wide, F32), V(wide, F32),
+        *three(2, 2, 2), *three(3, 2), V(wide, F32), V(wide, F32),
         pltpu.SemaphoreType.DMA((6, 2)), pltpu.SemaphoreType.DMA((6, 2)),
         pltpu.SemaphoreType.DMA((4, 3)), pltpu.SemaphoreType.DMA((4, 3)),
         pltpu.SemaphoreType.DMA((2,)), pltpu.SemaphoreType.DMA((2,)),

time: 761 us -> 761 us (level)
  no operation moved by 1% of the time
where the time goes in v4:
time: 761 us
  Pallas kernels  760 us (100%)
    pallas_call x1, Pallas kernels, fused(): pl.pallas_call(kernel, name='mlp_backward', out_shape=tuple((V(r.shape, r...  755 us

profile of v4, /device:TPU:0, one launch (start us, length us, event | category | flops | bytes accessed | tf_op | source)
XLA Modules:
  0.0 760.9 jit_solution(16491668085261659050)
XLA Ops:
  0.6 755.3 %mlp_backward.1 = (f32[3,56,4864]{2,1,0:T(8,128)S(1)}, f32[3,56,4864]{2,1,0:T(8,128)S(1)}, f32[3,304,896]{2,1,0:T(8,128)S(1)}, bf16[2048,896]{1,0:T(8,128)(2,1)S(1)}) custom-call(bf16[3,2048,896]{2,1,0:T(8,128)(2,1)} %h_hbm.1, bf16[2048,896]{1,0:T(8,128)(2,1)} %g_hbm.1, bf16[3,56,4864]{2,1,0:T(8,128)(2,1)} %w1_hbm.1, bf16[3,56,4864]{2,1,0:T(8,128)(2,1)} %w3_hbm.1, ...), custom_call_target="tpu_custom_call" | custom-call | tf_op jit(solution)/shard_map/mlp_backward/pallas_call | solution.py:493
  756.0 4.9 hand_out.1

commit v5 on v4

--- a/solution.py
+++ b/solution.py
@@ -113,7 +113,7 @@
     def half_copy(m, k):
         par = lax.rem(k, 2)
         return pltpu.make_async_remote_copy(
-            src_ref=halves[m].at[par, 1 - c], dst_ref=theirs[m].at[par], send_sem=ex_send.at[par], recv_sem=ex_recv.at[par],
+            src_ref=halves[m].at[lax.rem(k, 3), 1 - c], dst_ref=theirs[m].at[par], send_sem=ex_send.at[par], recv_sem=ex_recv.at[par],
             device_id=(core,), device_id_type=MESH)
 
     lane = lax.broadcasted_iota(jnp.int32, (DS, LANES), 1)
@@ -132,12 +132,12 @@
                     tile, off = place(half * (DEV // 2) + q, i)
                     part = pltpu.roll(cols[m][:, tile].astype(F32), lax.rem(CPD * q + LANES - off, LANES), 1)
                     acc = jnp.where((lane >= CPD * q) & (lane < CPD * (q + 1)), part, acc)
-                halves[m][lax.rem(k, 2), half] = acc
+                halves[m][lax.rem(k, 3), half] = acc
 
     def merge_rows(k):
         par = lax.rem(k, 2)
         for m in range(2):
-            mine, other = halves[m][par, c], theirs[m][par]
+            mine, other = halves[m][lax.rem(k, 3), c], theirs[m][par]
             low = jnp.where(c == 0, mine, other)
             high = jnp.where(c == 0, other, mine)
             weights[m][lax.rem(k, WS), c, z, y, x] = jnp.concatenate([low, high], axis=0).astype(BF)
@@ -246,14 +246,18 @@
                 gather_copy(m, 0, k + 4).start()
             own_copy(k + 4).start()
 
-        @pl.when((k <= 0) & (k > -LEAD))
-        def _():
-            pick_columns(k + 5)
-
         @pl.when(k + 5 < NK)
         def _():
             for m in range(2):
                 half_copy(m, k + 5).start()
+
+        @pl.when(k < -3)
+        def _():
+            pick_columns(k + 6)
+
+        @pl.when((k >= -4) & (k < -1))
+        def _():
+            pick_columns(k + 7)
 
         @pl.when((k + 6 == NC) | (k + 6 == 2 * NC))
         def _():
@@ -471,7 +475,7 @@
     scratch = [
         V((ROWS, D), BF), V((D, ROWS), BF), V((D, ROWS), BF),
         V((ROWS, D), F32), V((HR, BB, D), BF), V((ROWS, CH), BF), V((ROWS, 2 * CH), BF),
-        V((DS, FF), BF), V((DS, FF), BF), V((2, 2, DS, LANES), F32), V((2, 2, DS, LANES), F32),
+        V((DS, FF), BF), V((DS, FF), BF), V((3, 2, DS, LANES), F32), V((3, 2, DS, LANES), F32),
         V((2, DS, LANES), F32), V((2, DS, LANES), F32),
         V((WS, 2, 2, 2, 2, 2 * DS, HALF), BF), V((WS, 2, 2, 2, 2, 2 * DS, HALF), BF), V((WS, 2, 2, 2, 2, CPD, D), BF),
         *three(2, 2, 2, 2, 2),

time: 761 us -> 761 us (level)
  no operation moved by 1% of the time
where the time goes in v5:
time: 761 us
  Pallas kernels  761 us (100%)
    pallas_call x1, Pallas kernels, fused(): pl.pallas_call(kernel, name='mlp_backward', out_shape=tuple((V(r.shape, r...  756 us

profile of v5, /device:TPU:0, one launch (start us, length us, event | category | flops | bytes accessed | tf_op | source)
XLA Modules:
  0.0 761.2 jit_solution(474584541811539791)
XLA Ops:
  0.6 755.6 %mlp_backward.1 = (f32[3,56,4864]{2,1,0:T(8,128)S(1)}, f32[3,56,4864]{2,1,0:T(8,128)S(1)}, f32[3,304,896]{2,1,0:T(8,128)S(1)}, bf16[2048,896]{1,0:T(8,128)(2,1)S(1)}) custom-call(bf16[3,2048,896]{2,1,0:T(8,128)(2,1)} %h_hbm.1, bf16[2048,896]{1,0:T(8,128)(2,1)} %g_hbm.1, bf16[3,56,4864]{2,1,0:T(8,128)(2,1)} %w1_hbm.1, bf16[3,56,4864]{2,1,0:T(8,128)(2,1)} %w3_hbm.1, ...), custom_call_target="tpu_custom_call" | custom-call | tf_op jit(solution)/shard_map/mlp_backward/pallas_call | solution.py:497
  756.2 4.9 hand_out.1
